TPU v7x, 16 devices: a 4x2x1 block of a 4x4x8 slice. The times are simulated.
16 devices in a mesh: dp: 2 (over y, z), tp: 8 (over x, core).
Axes of the slice: x: 4, y: 2, z: 1, core: 2. Of those that a mesh axis runs over, the one named last changes fastest.
The devices are a block of a 4x4x8 slice.
Arguments:
- hidden: bfloat16 [2048, 4544], P(('dp', 'tp')), parts along dimension 0
- positions: int32 [2048], P(('dp', 'tp')), parts along dimension 0
- ln_gamma: float32 [2, 4544], replicated
- ln_beta: float32 [2, 4544], replicated
- w_qkv: bfloat16 [2, 4544, 4672], replicated
- w_out: bfloat16 [2, 4544, 4544], replicated
- w_up: bfloat16 [2, 4544, 18176], P(None, None, 'tp')
- w_down: bfloat16 [2, 18176, 4544], P(None, 'tp')
- k_cache: bfloat16 [2, 2048, 256, 64], P(None, ('dp', 'tp')), parts along dimension 1
- v_cache: bfloat16 [2, 2048, 256, 64], P(None, ('dp', 'tp')), parts along dimension 1
Outputs:
- output 1: bfloat16 [2048, 4544], P(('dp', 'tp')), parts along dimension 0
- output 2: bfloat16 [2, 2048, 256, 64], P(None, ('dp', 'tp')), parts along dimension 1
- output 3: bfloat16 [2, 2048, 256, 64], P(None, ('dp', 'tp')), parts along dimension 1
There are 2 independent parts. A program takes and returns all parts, laid end to end along the dimension named above; an argument that names none is the same for every part.
All inputs are finite; a program needn't handle non-finite values.
Results may differ from a plain program's by a relative error of at most 0.0126439.
Values are sent between devices in bfloat16 or wider.
A program may use at most 768 MiB of HBM per device.

v0:
```python
import jax
import jax.numpy as jnp
from jax import lax
from jax.sharding import PartitionSpec as P

LN_EPS = 1e-5
ROPE_BASE = 10000.0


def layer_norm(rows_in, gamma_row, beta_row):
    values = rows_in.astype(jnp.float32)
    row_mean = jnp.mean(values, axis=-1, keepdims=True)
    centered = values - row_mean
    variance = jnp.mean(centered * centered, axis=-1, keepdims=True)
    return (centered * lax.rsqrt(variance + LN_EPS) * gamma_row + beta_row).astype(jnp.bfloat16)


def rotary(vectors, positions):
    head_dim = vectors.shape[-1]
    half_dim = head_dim // 2
    inv_freq = 1.0 / (ROPE_BASE ** (jnp.arange(half_dim, dtype=jnp.float32) * (2.0 / head_dim)))
    angles = positions.astype(jnp.float32)[:, None] * inv_freq[None, :]
    cos_table = jnp.cos(angles)[:, None, :]
    sin_table = jnp.sin(angles)[:, None, :]
    first_half = vectors[..., :half_dim]
    second_half = vectors[..., half_dim:]
    return jnp.concatenate([first_half * cos_table - second_half * sin_table, second_half * cos_table + first_half * sin_table], axis=-1)


def local_attention(qkv_rows, positions, k_rows, v_rows):
    rows_n, seq_len, head_dim = k_rows.shape
    att_width = qkv_rows.shape[1] - 2 * head_dim
    num_heads = att_width // head_dim
    qkv_float = qkv_rows.astype(jnp.float32)
    query_rot = rotary(qkv_float[:, :att_width].reshape(rows_n, num_heads, head_dim), positions).astype(jnp.bfloat16)
    key_rot = rotary(qkv_float[:, att_width:att_width + head_dim].reshape(rows_n, 1, head_dim), positions).astype(jnp.bfloat16)
    value_new = qkv_rows[:, None, att_width + head_dim:]
    seq_ids = jnp.arange(seq_len, dtype=jnp.int32)
    write_mask = seq_ids[None, :, None] == positions[:, None, None]
    k_upd = jnp.where(write_mask, key_rot, k_rows)
    v_upd = jnp.where(write_mask, value_new, v_rows)
    scores = jnp.einsum('bhd,bsd->bhs', query_rot, k_upd, preferred_element_type=jnp.float32) * (head_dim ** -0.5)
    scores = jnp.where(seq_ids[None, None, :] <= positions[:, None, None], scores, -1e30)
    probabilities = jax.nn.softmax(scores, axis=-1).astype(jnp.bfloat16)
    context = jnp.einsum('bhs,bsd->bhd', probabilities, v_upd, preferred_element_type=jnp.float32)
    return context.astype(jnp.bfloat16).reshape(rows_n, att_width), k_upd, v_upd


def device_layers(hidden, positions, ln_gamma, ln_beta, w_qkv, w_out, w_up, w_down, k_cache, v_cache):
    hidden_state = hidden
    k_list = []
    v_list = []
    for layer_idx in range(w_qkv.shape[0]):
        normed = layer_norm(hidden_state, ln_gamma[layer_idx], ln_beta[layer_idx])
        qkv_rows = jnp.dot(normed, w_qkv[layer_idx], preferred_element_type=jnp.float32).astype(jnp.bfloat16)
        context, k_upd, v_upd = local_attention(qkv_rows, positions, k_cache[layer_idx], v_cache[layer_idx])
        attn_out = jnp.dot(context, w_out[layer_idx], preferred_element_type=jnp.float32).astype(jnp.bfloat16)
        normed_group = lax.all_gather(normed, 'tp', axis=0, tiled=True)
        activated = jax.nn.gelu(jnp.dot(normed_group, w_up[layer_idx], preferred_element_type=jnp.float32), approximate=False).astype(jnp.bfloat16)
        partial_sum = jnp.dot(activated, w_down[layer_idx], preferred_element_type=jnp.float32).astype(jnp.bfloat16)
        mlp_rows = lax.psum_scatter(partial_sum, 'tp', scatter_dimension=0, tiled=True)
        hidden_state = (hidden_state.astype(jnp.float32) + attn_out.astype(jnp.float32) + mlp_rows.astype(jnp.float32)).astype(jnp.bfloat16)
        k_list.append(k_upd)
        v_list.append(v_upd)
    return hidden_state, jnp.stack(k_list), jnp.stack(v_list)


def solution(mesh):
    row_spec = P(('dp', 'tp'), None)
    cache_spec = P(None, ('dp', 'tp'), None, None)
    in_specs = (row_spec, P(('dp', 'tp')), P(), P(), P(), P(), P(None, None, 'tp'), P(None, 'tp', None), cache_spec, cache_spec)
    return jax.shard_map(device_layers, mesh=mesh, in_specs=in_specs, out_specs=(row_spec, cache_spec, cache_spec), check_vma=False)
```

profile of v0, /device:TPU:113, one launch (start us, length us, event | category | flops | bytes accessed | tf_op | source)
XLA Modules:
  0.0 517.3 jit_solution(7991324988385331772)
XLA Ops:
  7.2 1.9 convert_reduce_fusion
  9.1 1.9 fusion.117
  11.0 1.7 slice_reduce_fusion
  12.7 4.5 fusion.120
  17.3 56.2 %all-gather.3.cloned.1.call-done = bf16[1024,4544]{0,1:T(8,128)(2,1)} async-done(((bf16[128,4544]{0,1:T(8,128)(2,1)}), bf16[1024,4544]{0,1:T(8,128)(2,1)}) %all-gather.3.cloned.1.call-update) | async-done | bytes 9306128 | tf_op jit(solution)/shard_map/all_gather | solution.py:58
  73.5 61.2 %fusion.34 = bf16[1024,2272]{0,1:T(8,128)(2,1)S(1)} fusion(bf16[1024,4544]{0,1:T(8,128)(2,1)} %all-gather.3.cloned.1.call-done, bf16[2,4544,2272]{2,1,0:T(8,128)(2,1)} %param.16), kind=kOutput, calls=%fused_computation.38 | convolution fusion | flops 21294710784 | bytes 34897920 | tf_op jit(solution)/shard_map/dot_general | solution.py:59
  134.7 27.4 %fusion.26 = bf16[1024,4544]{0,1:T(8,128)(2,1)} fusion(bf16[1024,2272]{0,1:T(8,128)(2,1)S(1)} %fusion.34, bf16[2,2272,4544]{2,1,0:T(8,128)(2,1)} %param.17), kind=kOutput, calls=%fused_computation.28 | convolution fusion | flops 21148139520 | bytes 34897920 | tf_op jit(solution)/shard_map/dot_general | solution.py:60
  162.1 12.5 %copy.53 = bf16[1024,4544]{1,0:T(8,128)(2,1)} copy(bf16[1024,4544]{0,1:T(8,128)(2,1)} %fusion.26) | data formatting | bytes 18612224
  174.8 1.1 copy-done.3
  175.9 24.3 %fusion.161 = (f32[128,4672]{0,1:T(8,128)}, bf16[128,4672]{0,1:T(8,128)(2,1)S(1)}) fusion(bf16[128,4544]{0,1:T(8,128)(2,1)S(1)} %copy-done.3, bf16[2,4544,4672]{2,1,0:T(8,128)(2,1)} %param.14), kind=kOutput, calls=%fused_computation.188 | convolution fusion | flops 5435965440 | bytes 47792128 | tf_op jit(solution)/shard_map/dot_general | solution.py:55
  201.0 0.8 slice_bitcast_fusion.1
  202.1 0.8 copy.42
  203.0 1.3 fusion.160
  204.2 2.4 copy.58
  206.6 2.1 copy.57
  208.7 0.8 iota_compare_fusion.1
  209.4 1.0 multiply_cosine_fusion
  210.5 3.3 subtract_convert_fusion.1
  213.8 4.7 fusion.106
  218.5 7.0 %fusion.162 = (f32[128,71]{1,0:T(8,128)S(1)}, f32[128,71,256]{2,1,0:T(8,128)}) fusion(f32[128,71,256]{2,1,0:T(8,128)S(1)} %fusion.106, pred[128,256]{1,0:T(8,128)(4,1)S(1)} %get-tuple-element.27), kind=kOutput, calls=%fused_computation.189 | output fusion | flops 13959423 | bytes 18681344 | tf_op jit(solution)/shard_map/sub | solution.py:44
  225.5 6.5 %fusion.132 = bf16[128,71,64]{1,2,0:T(8,128)(2,1)S(1)} fusion(pred[128,256]{1,0:T(8,128)(4,1)S(1)} %get-tuple-element.28, bf16[2,128,256,64]{2,3,1,0:T(8,128)(2,1)} %param.19, bf16[128,64]{1,0:T(8,128)(2,1)S(1)} %copy.42, f32[128,71,256]{2,1,0:T(8,128)} %get-tuple-element.32, f32[128,71]{1,0:T(8,128)S(1)} %get-tuple-element.31), kind=kOutput, calls=%fused_computation.140 | convolution fusion | flops 305127424 | bytes 14880256 | tf_op jit(solution)/shard_map/bhs,bsd->bhd/dot_general | solution.py:45
  232.0 3.0 copy.43
  234.9 2.4 copy.54
  237.3 19.3 %fusion.163 = (f32[128]{0:T(128)S(1)}, f32[128,4544]{0,1:T(8,128)S(1)}) fusion(bf16[128,4544]{0,1:T(8,128)(2,1)} %copy.54, bf16[128,4544]{0,1:T(8,128)(2,1)} %bitcast.109, bf16[2,4544,4544]{2,1,0:T(8,128)(2,1)} %param.15, bf16[128,4544]{0,1:T(8,128)(2,1)S(1)} %copy-done), kind=kOutput, calls=%fused_computation.190 | convolution fusion | flops 5291106304 | bytes 47694336 | tf_op jit(solution)/shard_map/dot_general | solution.py:57
  256.6 0.6 multiply_reduce_fusion
  257.3 3.2 add_convert_fusion
  260.6 53.8 %all-gather.5.cloned.1.call-done = bf16[1024,4544]{0,1:T(8,128)(2,1)} async-done(((bf16[128,4544]{0,1:T(8,128)(2,1)}), bf16[1024,4544]{0,1:T(8,128)(2,1)}) %all-gather.5.cloned.1.call-update) | async-done | bytes 9306128 | tf_op jit(solution)/shard_map/all_gather | solution.py:58
  314.5 48.7 %fusion.37 = bf16[1024,2272]{0,1:T(8,128)(2,1)S(1)} fusion(bf16[1024,4544]{0,1:T(8,128)(2,1)} %all-gather.5.cloned.1.call-done, bf16[2,4544,2272]{2,1,0:T(8,128)(2,1)} %param.16), kind=kOutput, calls=%fused_computation.41 | convolution fusion | flops 21294710784 | bytes 34897920 | tf_op jit(solution)/shard_map/dot_general | solution.py:59
  363.2 27.4 %fusion.29 = bf16[1024,4544]{0,1:T(8,128)(2,1)} fusion(bf16[1024,2272]{0,1:T(8,128)(2,1)S(1)} %fusion.37, bf16[2,2272,4544]{2,1,0:T(8,128)(2,1)} %param.17), kind=kOutput, calls=%fused_computation.29 | convolution fusion | flops 21148139520 | bytes 34897920 | tf_op jit(solution)/shard_map/dot_general | solution.py:60
  390.6 12.5 %copy.55 = bf16[1024,4544]{1,0:T(8,128)(2,1)} copy(bf16[1024,4544]{0,1:T(8,128)(2,1)} %fusion.29) | data formatting | bytes 18612224
  403.2 1.2 copy-done.4
  404.4 24.3 %fusion.164 = (f32[128,4672]{0,1:T(8,128)}, bf16[128,4672]{0,1:T(8,128)(2,1)S(1)}) fusion(bf16[128,4544]{0,1:T(8,128)(2,1)S(1)} %copy-done.4, bf16[2,4544,4672]{2,1,0:T(8,128)(2,1)} %param.14), kind=kOutput, calls=%fused_computation.191 | convolution fusion | flops 5435965440 | bytes 47792128 | tf_op jit(solution)/shard_map/dot_general | solution.py:55
  428.7 0.6 slice.133
  429.5 0.8 slice_bitcast_fusion
  430.5 1.4 copy.47
  432.0 1.2 fusion.159
  433.2 2.4 copy.60
  435.6 2.1 copy.59
  437.7 3.6 subtract_convert_fusion
  441.3 4.7 fusion.105
  446.0 6.9 %fusion.165 = (f32[128,71]{1,0:T(8,128)S(1)}, f32[128,71,256]{2,1,0:T(8,128)}) fusion(f32[128,71,256]{2,1,0:T(8,128)S(1)} %fusion.105, pred[128,256]{1,0:T(8,128)(4,1)S(1)} %copy-done.17), kind=kOutput, calls=%fused_computation.192 | output fusion | flops 13959423 | bytes 18681344 | tf_op jit(solution)/shard_map/sub | solution.py:44
  453.0 6.4 %fusion.131 = bf16[128,71,64]{1,2,0:T(8,128)(2,1)S(1)} fusion(pred[128,256]{1,0:T(8,128)(4,1)S(1)} %copy-done.8, bf16[2,128,256,64]{2,3,1,0:T(8,128)(2,1)} %param.19, bf16[128,64]{1,0:T(8,128)(2,1)S(1)} %copy-done.13, f32[128,71,256]{2,1,0:T(8,128)} %get-tuple-element.38, f32[128,71]{1,0:T(8,128)S(1)} %get-tuple-element.37), kind=kOutput, calls=%fused_computation.139 | convolution fusion | flops 305127424 | bytes 14880256 | tf_op jit(solution)/shard_map/bhs,bsd->bhd/dot_general | solution.py:45
  459.4 3.0 copy.48
  462.4 11.7 %broadcast_select_fusion.1 = (bf16[1,128,256,64]{2,3,1,0:T(8,128)(2,1)}, bf16[1,128,256,64]{2,3,1,0:T(8,128)(2,1)}, bf16[1,128,256,64]{2,3,1,0:T(8,128)(2,1)S(1)}, bf16[1,128,256,64]{2,3,1,0:T(8,128)(2,1)}) fusion(pred[128,256]{1,0:T(8,128)(4,1)S(1)} %copy-done.8, bf16[2,128,256,64]{2,3,1,0:T(8,128)(2,1)} %param.19, bf16[128,64]{1,0:T(8,128)(2,1)S(1)} %copy-done.12, ...), kind=kLoop, calls=%fused_computation.104 | loop fusion | flops 8388608 | bytes 33652736 | tf_op jit(solution)/shard_map/jit(_where)/select_n | solution.py:41
  474.1 7.6 %pad_maximum_fusion.1 = bf16[2,128,256,64]{2,3,1,0:T(8,128)(2,1)} fusion(bf16[1,128,256,64]{2,3,1,0:T(8,128)(2,1)} %get-tuple-element.8, bf16[1,128,256,64]{2,3,1,0:T(8,128)(2,1)} %get-tuple-element.7), kind=kLoop, calls=%fused_computation.73 | loop fusion | flops 4194304 | bytes 16777216 | tf_op jit(solution)/shard_map/stack | solution.py:65
  481.7 6.5 %pad_maximum_fusion = bf16[2,128,256,64]{2,3,1,0:T(8,128)(2,1)} fusion(bf16[1,128,256,64]{2,3,1,0:T(8,128)(2,1)S(1)} %get-tuple-element.23, bf16[1,128,256,64]{2,3,1,0:T(8,128)(2,1)} %get-tuple-element.24), kind=kLoop, calls=%fused_computation.72 | loop fusion | flops 4194304 | bytes 16777216 | tf_op jit(solution)/shard_map/stack | solution.py:65
  488.2 2.4 copy.56
  490.6 20.0 %fusion.78 = bf16[128,4544]{0,1:T(8,128)(2,1)} fusion(f32[128,4544]{0,1:T(8,128)S(1)} %copy-done.2, bf16[128,4544]{0,1:T(8,128)(2,1)} %bitcast.108, bf16[2,4544,4544]{2,1,0:T(8,128)(2,1)} %param.15, bf16[128,4544]{0,1:T(8,128)(2,1)} %copy.56), kind=kOutput, calls=%fused_computation.84 | convolution fusion | flops 5289361408 | bytes 47693824 | tf_op jit(solution)/shard_map/dot_general | solution.py:57
  (69 shorter events, 2.0 us)
Async XLA Ops:
  7.2 66.4 %all-gather.3.cloned.1.call-start = ((), (), s32[]{:S(2)}) async-start(), calls=%async_computation.2 | async-start | bytes 10469376 | tf_op jit(solution)/shard_map/all_gather | solution.py:58
  17.2 217.7 %reduce-scatter.7.cloned.1.call-start = ((), (), s32[]{:S(2)}) async-start(), calls=%async_computation.4 | async-start | bytes 10616832
  174.6 1.3 copy-start.3
  174.7 26.3 %copy-start.22 = (s32[128]{0:T(128)S(1)}, s32[128]{0:T(128)}, u32[]{:S(2)}) copy-start(s32[128]{0:T(128)} %param.11) | copy-start | bytes 1540
  174.7 139.8 %all-gather.5.cloned.1.call-start = ((), (), s32[]{:S(2)}) async-start(), calls=%async_computation.3 | async-start | bytes 10469376 | tf_op jit(solution)/shard_map/all_gather | solution.py:58
  201.0 0.9 copy-start.18
  201.0 0.9 copy-start.20
  202.1 16.4 %copy-start.9 = (bf16[128,64]{1,0:T(8,128)(2,1)}, bf16[128,64]{1,0:T(8,128)(2,1)S(1)}, u32[]{:S(2)}) copy-start(bf16[128,64]{1,0:T(8,128)(2,1)S(1)} %copy.41) | copy-start | bytes 49156
  203.0 22.5 %copy-start.11 = (bf16[128,64]{1,0:T(8,128)(2,1)}, bf16[128,64]{1,0:T(8,128)(2,1)S(1)}, u32[]{:S(2)}) copy-start(bf16[128,64]{1,0:T(8,128)(2,1)S(1)} %copy.42) | copy-start | bytes 49156
  209.4 9.1 %copy-start.16 = (pred[128,256]{1,0:T(8,128)(4,1)}, pred[128,256]{1,0:T(8,128)(4,1)S(1)}, u32[]{:S(2)}) copy-start(pred[128,256]{1,0:T(8,128)(4,1)S(1)} %get-tuple-element.27) | copy-start | bytes 98308
  209.4 16.1 %copy-start.7 = (pred[128,256]{1,0:T(8,128)(4,1)}, pred[128,256]{1,0:T(8,128)(4,1)S(1)}, u32[]{:S(2)}) copy-start(pred[128,256]{1,0:T(8,128)(4,1)S(1)} %get-tuple-element.28) | copy-start | bytes 98308
  210.4 8.1 %copy-start.5 = (f32[128,32]{1,0:T(8,128)}, f32[128,32]{1,0:T(8,128)S(1)}, u32[]{:S(2)}) copy-start(f32[128,32]{1,0:T(8,128)S(1)} %get-tuple-element.25) | copy-start | bytes 49156
  210.4 8.1 %copy-start.6 = (f32[128,32]{1,0:T(8,128)}, f32[128,32]{1,0:T(8,128)S(1)}, u32[]{:S(2)}) copy-start(f32[128,32]{1,0:T(8,128)S(1)} %get-tuple-element.26) | copy-start | bytes 49156
  225.5 11.8 %copy-start = (bf16[128,4544]{0,1:T(8,128)(2,1)S(1)}, bf16[128,4544]{0,1:T(8,128)(2,1)}, u32[]{:S(2)}) copy-start(bf16[128,4544]{0,1:T(8,128)(2,1)} %param.10) | copy-start | bytes 3489796
  237.3 20.0 %copy-start.14 = (f32[4544]{0:T(1024)S(1)}, f32[4544]{0:T(1024)}, u32[]{:S(2)}) copy-start(f32[4544]{0:T(1024)} %get-tuple-element.5) | copy-start | bytes 54532
  237.3 20.0 %copy-start.15 = (f32[4544]{0:T(1024)S(1)}, f32[4544]{0:T(1024)}, u32[]{:S(2)}) copy-start(f32[4544]{0:T(1024)} %get-tuple-element.40) | copy-start | bytes 54532
  256.6 106.6 %copy-start.1 = (f32[128,4544]{0,1:T(8,128)}, f32[128,4544]{0,1:T(8,128)S(1)}, u32[]{:S(2)}) copy-start(f32[128,4544]{0,1:T(8,128)S(1)} %get-tuple-element.34) | copy-start | bytes 6979588
  260.6 227.6 %reduce-scatter.9.cloned.1.call-start = ((), (), s32[]{:S(2)}) async-start(), calls=%async_computation.5 | async-start | bytes 10616832
  403.1 1.3 copy-start.4
  404.4 25.9 %copy-start.19 = (f32[128]{0:T(128)S(1)}, f32[128]{0:T(128)}, u32[]{:S(2)}) copy-start(f32[128]{0:T(128)} %copy-done.18) | copy-start | bytes 1540
  404.4 25.9 %copy-start.21 = (f32[32]{0:T(128)S(1)}, f32[32]{0:T(128)}, u32[]{:S(2)}) copy-start(f32[32]{0:T(128)} %copy-done.20) | copy-start | bytes 388
  429.5 11.8 %copy-start.8 = (pred[128,256]{1,0:T(8,128)(4,1)S(1)}, pred[128,256]{1,0:T(8,128)(4,1)}, u32[]{:S(2)}) copy-start(pred[128,256]{1,0:T(8,128)(4,1)} %copy-done.7) | copy-start | bytes 98308
  441.3 4.7 copy-start.17
  446.0 6.9 %copy-start.13 = (bf16[128,64]{1,0:T(8,128)(2,1)S(1)}, bf16[128,64]{1,0:T(8,128)(2,1)}, u32[]{:S(2)}) copy-start(bf16[128,64]{1,0:T(8,128)(2,1)} %copy.47) | copy-start | bytes 49156
  453.0 9.4 %copy-start.10 = (bf16[128,64]{1,0:T(8,128)(2,1)S(1)}, bf16[128,64]{1,0:T(8,128)(2,1)}, u32[]{:S(2)}) copy-start(bf16[128,64]{1,0:T(8,128)(2,1)} %copy-done.9) | copy-start | bytes 49156
  453.0 9.4 %copy-start.12 = (bf16[128,64]{1,0:T(8,128)(2,1)S(1)}, bf16[128,64]{1,0:T(8,128)(2,1)}, u32[]{:S(2)}) copy-start(bf16[128,64]{1,0:T(8,128)(2,1)} %copy-done.11) | copy-start | bytes 49156
  481.7 8.9 %copy-start.2 = (f32[128,4544]{0,1:T(8,128)S(1)}, f32[128,4544]{0,1:T(8,128)}, u32[]{:S(2)}) copy-start(f32[128,4544]{0,1:T(8,128)} %copy-done.1) | copy-start | bytes 6979588
Sparse Core Ops, SparseCore 0:
  17.4 56.1 all-gather.2
  174.8 53.4 reduce-scatter.6
  260.7 53.7 all-gather.4
  403.3 53.4 reduce-scatter.8
where the time goes:
time: 521 us; the launch traced here: 517 us
  matrix products  275 us (53%)
  waiting for transfers between devices  110 us (21%)
  other arithmetic  60.8 us (12%)
  local copies, waits for them, and re-layouts  56.7 us (11%)
  between operations  14.4 us (3%)
    all_gather x2, waiting for transfers between devices, device_layers(): normed_group = lax.all_gather(normed, 'tp', axis=0, tiled=True)  110 us
    dot_general x2, matrix products, device_layers(): jnp.dot(normed_group, w_up[layer_idx], preferred_element_type=jnp.float32)  110 us
    dot_general x2, matrix products, device_layers(): jnp.dot(activated, w_down[layer_idx], preferred_element_type=jnp.float32)  54.8 us
    dot_general x2, matrix products, device_layers(): jnp.dot(normed, w_qkv[layer_idx], preferred_element_type=jnp.float32)  48.7 us
    unnamed x54, local copies, waits for them, and re-layouts  41 us
    dot_general x2, matrix products, device_layers(): jnp.dot(context, w_out[layer_idx], preferred_element_type=jnp.float32)  39.3 us
    another operation x2, other arithmetic, device_layers(): return (hidden_state, jnp.stack(k_list), jnp.stack(v_list))  14.1 us
    sub x2, other arithmetic, local_attention(): probabilities = jax.nn.softmax(scores, axis=-1).astype(jnp.bfloat16)  13.9 us
  transfers between devices with their start and end apart: 4, of which 2 were waited for; matrix products, arithmetic and copies ran while one was open for 28% of the time, Pallas kernels for 0%

commit v1 on v0

v1 whole, which is shorter than its diff:
```python
import functools

import jax
import jax.numpy as jnp
from jax import lax
from jax.experimental import pallas as pl
from jax.experimental.pallas import tpu as pltpu
from jax.sharding import PartitionSpec as P

LN_EPS = 1e-5
ROPE_BASE = 10000.0
CHUNK = 512
QKV_SLOTS = 3
ROW_BLOCK = 8
CACHE_SLOTS = 4
F32 = jnp.float32
BF16 = jnp.bfloat16


def span(index, step, size):
    if isinstance(index, int):
        return pl.ds(index * step, size)
    return pl.ds(pl.multiple_of(index * step, step), size)


def gelu(u):
    return 0.5 * u * (1.0 + lax.erf(u * (2.0 ** -0.5)))


def layer_kernel(layer, last, h_ref, pos_ref, cs_ref, x_ref, gb_ref, w_qkv, k_cache, v_cache, w_up, w_down, w_out, *refs):
    hg, kv_ref, xo_ref, *refs = refs
    (ho_ref, wup, wtail, kv, hb, act, u_ref, mine, sib_send, sib_recv, sbuf, rbuf,
     w_sem, t_sem, kv_sem, own_sem, rs_sem, rr_sem, as_sem, ar_sem,
     u_sem, d_sem, h_sem, o_sem, x_sem, ss_sem, sr_sem, is_sem, ir_sem) = refs
    ctx_ref = ho_ref
    rows, width = h_ref.shape
    total = w_qkv.shape[2]
    head_dim, seq_len = k_cache.shape[2:]
    stride = pair_stride(width)
    n_chunks = total // CHUNK
    tail = total - n_chunks * CHUNK
    pairs = CHUNK // 128
    n_blocks = rows // ROW_BLOCK
    half = rows // 2
    scale = head_dim ** -0.5
    ff = w_up.shape[2]
    n_up = -(-ff // CHUNK)
    n_dn = -(-width // CHUNK)
    up_tail = ff - (n_up - 1) * CHUNK
    dn_tail = width - (n_dn - 1) * CHUNK
    size = lax.axis_size("tp")
    chips = size // 2
    me = lax.axis_index("tp")
    core = lax.rem(me, 2)
    chip = lax.div(me, 2)
    sib = 2 * chip + 1 - core
    left = 2 * lax.rem(chip + chips - 1, chips) + core
    right = 2 * lax.rem(chip + 1, chips) + core
    far = 2 * lax.rem(chip + 2, chips) + core
    n_left = n_dn // 2 + 1 - core

    def part(owner, which):
        return hg.at[pl.ds(pl.multiple_of(owner * rows + which * half, half), half)]

    def whole(owner):
        return hg.at[pl.ds(pl.multiple_of(owner * rows, rows), rows)]

    def remote(src, dst, send, recv, to):
        return pltpu.make_async_remote_copy(
            src_ref=src, dst_ref=dst, send_sem=send, recv_sem=recv,
            device_id={"tp": to}, device_id_type=pl.DeviceIdType.MESH)

    def to_right(i):
        if i == 2:
            return remote(part(left, 0), part(left, 0), rs_sem.at[0, 2], rr_sem.at[0, 2], right)
        return remote(h_ref.at[pl.ds(i * half, half)], part(me, i), rs_sem.at[0, i], rr_sem.at[0, i], right)

    def to_left(i):
        if i == 2:
            return remote(part(right, 1), part(right, 1), rs_sem.at[1, 2], rr_sem.at[1, 2], left)
        return remote(h_ref.at[pl.ds((1 - i) * half, half)], part(me, 1 - i), rs_sem.at[1, i], rr_sem.at[1, i], left)

    def to_sib(i):
        block = (None, lambda: whole(left), lambda: whole(right), lambda: part(far, 0), lambda: part(far, 1))[i]
        src = h_ref if i == 0 else block()
        dst = whole(me) if i == 0 else block()
        return remote(src, dst, as_sem.at[i], ar_sem.at[i], sib)

    own_copy = pltpu.make_async_copy(h_ref, whole(me), own_sem)

    def up_copy(j, w):
        cols = span(j, CHUNK, w)
        return pltpu.make_async_copy(w_up.at[layer, :, cols], wup.at[:, cols], u_sem.at[j])

    def attention_scope(wbuf, qp, kbuf, vbuf):
        def w_copy(j):
            cols = span(j, CHUNK, CHUNK)
            slot = j % QKV_SLOTS if isinstance(j, int) else lax.rem(j, QKV_SLOTS)
            return pltpu.make_async_copy(w_qkv.at[layer, :, cols], wbuf.at[slot], w_sem.at[slot])

        def qkv_tail_copy():
            return pltpu.make_async_copy(w_qkv.at[layer, :, pl.ds(n_chunks * CHUNK, tail)], wtail, t_sem)

        def cache_copies(i):
            slot = lax.rem(i, CACHE_SLOTS)
            at = span(i, ROW_BLOCK, ROW_BLOCK)
            return (pltpu.make_async_copy(k_cache.at[layer, at], kbuf.at[slot], kv_sem.at[0, slot]),
                    pltpu.make_async_copy(v_cache.at[layer, at], vbuf.at[slot], kv_sem.at[1, slot]))

        barrier = pltpu.get_barrier_semaphore()
        for other in (sib, left, right):
            pl.semaphore_signal(barrier, inc=1, device_id={"tp": other}, device_id_type=pl.DeviceIdType.MESH)
        for j in range(QKV_SLOTS):
            w_copy(j).start()
        qkv_tail_copy().start()
        own_copy.start()
        pl.semaphore_wait(barrier, 3)
        for i in range(2):
            to_right(i).start()
            to_left(i).start()
        to_sib(0).start()

        lane = lax.broadcasted_iota(jnp.int32, (1, 128), 1)
        first = lax.rem(lane, head_dim) < head_dim // 2

        def rope(block):
            block = block.astype(BF16).astype(F32)
            ahead = pltpu.roll(block, 128 - head_dim // 2, 1)
            behind = pltpu.roll(block, head_dim // 2, 1)
            turned = block * cs_ref[0] + jnp.where(first, ahead, behind) * cs_ref[1]
            return turned.astype(BF16).astype(F32)

        def qkv_chunk(j):
            slot = j % QKV_SLOTS if isinstance(j, int) else lax.rem(j, QKV_SLOTS)
            w_copy(j).wait()
            return jnp.dot(h_ref[...], wbuf[slot], preferred_element_type=F32)

        @pl.loop(0, n_chunks - 1)
        def _(j):
            out = qkv_chunk(j)

            @pl.when(j + QKV_SLOTS < n_chunks)
            def _():
                w_copy(j + QKV_SLOTS).start()

            for i in range(pairs):
                qp[pl.ds(j * pairs + i, rows, stride), :] = rope(out[:, 128 * i:128 * (i + 1)])

        for i in range(CACHE_SLOTS):
            for cp_ in cache_copies(i):
                cp_.start()
        for j in range(n_up):
            up_copy(j, CHUNK if j < n_up - 1 else up_tail).start()
        out = qkv_chunk(n_chunks - 1)
        turned = None
        for i in range(pairs):
            turned = rope(out[:, 128 * i:128 * (i + 1)])
            qp[pl.ds((n_chunks - 1) * pairs + i, rows, stride), :] = turned
        qkv_tail_copy().wait()
        value = jnp.dot(h_ref[...], wtail[...], preferred_element_type=F32).astype(BF16).astype(F32)
        kv[...] = jnp.concatenate([turned[:, 128 - head_dim:], value], axis=1)
        kv_ref[...] = kv[...].astype(BF16)

        slots = lax.broadcasted_iota(jnp.int32, (1, seq_len), 1)

        def attend(i):
            slot = lax.rem(i, CACHE_SLOTS)
            for cp_ in cache_copies(i):
                cp_.wait()
            queries, scores, probs = [], [], []
            for r in range(ROW_BLOCK):
                b = i * ROW_BLOCK + r
                two = qp[pl.ds(pl.multiple_of(b * stride, 8), stride), :]
                query = jnp.concatenate([two[:, :head_dim], two[:, head_dim:]], axis=0)
                queries.append(query)
                scores.append(jnp.dot(query.astype(BF16), kbuf[slot, r], preferred_element_type=F32))
            for r in range(ROW_BLOCK):
                b = i * ROW_BLOCK + r
                at = pos_ref[b]
                key = kv[pl.ds(b, 1), :head_dim]
                new = jnp.sum(queries[r] * key, axis=1, keepdims=True) * scale
                score = jnp.where(slots < at, scores[r] * scale, -1e30)
                top = jnp.maximum(jnp.max(score, axis=1, keepdims=True), new)
                weight = jnp.exp(score - top)
                new_weight = jnp.exp(new - top)
                inverse = 1.0 / (jnp.sum(weight, axis=1, keepdims=True) + new_weight)
                probs.append(((weight * inverse).astype(BF16), (new_weight * inverse).astype(BF16).astype(F32)))
            for r in range(ROW_BLOCK):
                b = i * ROW_BLOCK + r
                old, new = probs[r]
                context = lax.dot_general(old, vbuf[slot, r], (((1,), (1,)), ((), ())), preferred_element_type=F32)
                context += new * kv[pl.ds(b, 1), head_dim:]
                to = pl.ds(pl.multiple_of(b * stride, 8), stride)
                qp[to, :] = jnp.concatenate([context[:stride], context[stride:]], axis=1)

            @pl.when(i + CACHE_SLOTS < n_blocks)
            def _():
                for cp_ in cache_copies(i + CACHE_SLOTS):
                    cp_.start()


        @pl.loop(0, n_blocks)
        def _(i):
            @pl.when(i == 1)
            def _():
                to_right(0).wait_recv()
                to_right(2).start()
                to_left(0).wait_recv()
                to_left(2).start()

            attend(i)

        for m in range(-(-width // 128)):
            w = min(128, width - 128 * m)
            ctx_ref[:, 128 * m:128 * m + w] = qp[pl.ds(m, rows, stride), :][:, :w].astype(BF16)

    pl.run_scoped(
        attention_scope,
        pltpu.VMEM((QKV_SLOTS, width, CHUNK), BF16),
        pltpu.VMEM((rows * stride, 128), F32),
        pltpu.VMEM((CACHE_SLOTS, ROW_BLOCK, head_dim, seq_len), BF16),
        pltpu.VMEM((CACHE_SLOTS, ROW_BLOCK, head_dim, seq_len), BF16),
    )

    to_right(1).wait_recv()
    to_sib(1).start()
    to_left(1).wait_recv()
    to_sib(2).start()
    own_copy.wait()
    to_sib(0).wait_recv()

    def mlp_scope(wdn):
        def dn_copy(k, w):
            cols = span(k, CHUNK, w)
            return pltpu.make_async_copy(w_down.at[layer, :, cols], wdn.at[:, cols], d_sem.at[k])

        def h_copies(t):
            off = jnp.where(t == 0, 0, jnp.where(t == 1, 2, jnp.where(t == 2, 1, chips - 1)))
            dest = lax.rem(chip + off, chips)
            first = pl.multiple_of((2 * dest + core) * rows, rows)
            second = pl.multiple_of((2 * dest + 1 - core) * rows, rows)
            return (
                pltpu.make_async_copy(hg.at[pl.ds(first, rows)], hb.at[pl.ds(0, rows)], h_sem.at[0]),
                pltpu.make_async_copy(hg.at[pl.ds(second, rows)], hb.at[pl.ds(rows, rows)], h_sem.at[1]),
            )

        def sib_copy(t, k):
            slot = lax.rem(t * n_dn + k, 4)
            return pltpu.make_async_remote_copy(
                src_ref=sib_send.at[slot], dst_ref=sib_recv.at[lax.rem(t, 2) * n_dn + k],
                send_sem=ss_sem.at[slot], recv_sem=sr_sem.at[t, k],
                device_id={"tp": sib}, device_id_type=pl.DeviceIdType.MESH)

        def sums(t):
            return jnp.where(t == 3, 1, t)

        def ring_copy(t, k):
            goes_right = jnp.logical_or(t == 2, jnp.logical_and(t == 1, k >= n_left))
            return pltpu.make_async_remote_copy(
                src_ref=sbuf.at[sums(t) * n_dn + k], dst_ref=rbuf.at[t - 1, k],
                send_sem=is_sem.at[t - 1, k], recv_sem=ir_sem.at[t - 1, k],
                device_id={"tp": jnp.where(goes_right, right, left)}, device_id_type=pl.DeviceIdType.MESH)

        def up_phase(t):
            for cp in h_copies(t):
                cp.wait()

            def ready(j, w):
                @pl.when(t == 0)
                def _():
                    up_copy(j, w).wait()

            def dot(j, w):
                cols = span(j, CHUNK, w)
                return jnp.dot(hb[...], wup[:, cols], preferred_element_type=F32)

            ready(0, CHUNK)
            u_ref[...] = dot(0, CHUNK)

            @pl.loop(1, n_up - 1)
            def _(j):
                ready(j, CHUNK)
                prev = span(j - 1, CHUNK, CHUNK)
                act[:, prev] = gelu(u_ref[...]).astype(BF16)
                u_ref[...] = dot(j, CHUNK)

            ready(n_up - 1, up_tail)
            act[:, (n_up - 2) * CHUNK:(n_up - 1) * CHUNK] = gelu(u_ref[...]).astype(BF16)
            cols = span(n_up - 1, CHUNK, up_tail)
            for half in (pl.ds(0, rows), pl.ds(rows, rows)):
                tail = jnp.dot(hb[half, :], wup[:, cols], preferred_element_type=F32)
                act[half, (n_up - 1) * CHUNK:] = gelu(tail).astype(BF16)

        def arrive(t, k):
            sib_copy(t, k).wait_recv()
            relay = jnp.logical_or(jnp.logical_and(t == 2, k >= n_left), jnp.logical_and(t == 3, k < n_left))

            @pl.when(relay)
            def _():
                ring_copy(1, k).wait_recv()
                mine[lax.rem(t * n_dn + k, 2)] += rbuf[0, k].astype(F32)

            @pl.when(t == 3)
            def _():
                ring_copy(1, k).wait_send()

        def settle(t, k, slot, spare):
            to = jnp.where(spare, 3 * n_dn, sums(t) * n_dn + k)
            of = jnp.where(spare, 2 * n_dn, lax.rem(t, 2) * n_dn + k)
            sbuf[to] = (mine[slot] + sib_recv[of].astype(F32)).astype(BF16)

        def down_phase(t):
            def dot(k, w):
                return jnp.dot(act[...], wdn[:, span(k, CHUNK, w)], preferred_element_type=F32)

            def step(k, w):
                q = t * n_dn + k
                pt = jnp.maximum(jnp.where(k < 2, t - 1, t), 0)
                pk = jnp.where(k < 2, k + n_dn - 2, k - 2)
                slot = lax.rem(q, 2)

                @pl.when(t == 0)
                def _():
                    dn_copy(k, w).wait()

                @pl.when(q >= 4)
                def _():
                    sib_copy(t, k).wait_send()

                @pl.when(q >= 2)
                def _():
                    arrive(pt, pk)

                settle(pt, pk, slot, q < 2)
                out = dot(k, w)
                mine[slot, :, :w] = out[:rows]
                sib_send[lax.rem(q, 4), :, :w] = out[rows:].astype(BF16)
                sib_copy(t, k).start()

                @pl.when(jnp.logical_and(q >= 2, pt > 0))
                def _():
                    ring_copy(pt, pk).start()

            @pl.loop(0, n_dn - 1)
            def _(k):
                step(k, CHUNK)

            step(n_dn - 1, dn_tail)


        def out_copy(j):
            slot = j % 4 if isinstance(j, int) else lax.rem(j, 4)
            w = min(CHUNK, out_full - j * CHUNK) if isinstance(j, int) else CHUNK
            return pltpu.make_async_copy(
                w_out.at[layer, :, span(j, CHUNK, w)], wup.at[:, span(slot, CHUNK, w)], o_sem.at[slot])

        def out_chunk(j, w):
            slot = j % 4 if isinstance(j, int) else lax.rem(j, 4)
            out_copy(j).wait()
            attn = jnp.dot(ctx_ref[...], wup[:, span(slot, CHUNK, w)], preferred_element_type=F32)
            hb[:rows, span(j, CHUNK, w)] = attn.astype(BF16)

        for cp_ in h_copies(0):
            cp_.start()
        for k in range(n_dn):
            dn_copy(k, CHUNK if k < n_dn - 1 else dn_tail).start()
        @pl.loop(0, 3)
        def _(t):
            up_phase(t)

            @pl.when(t > 0)
            def _():
                for cp_ in h_copies(t + 1):
                    cp_.start()

            down_phase(t)

            @pl.when(t == 0)
            def _():
                to_right(2).wait_recv()
                to_sib(3).start()
                to_left(2).wait_recv()
                to_sib(4).start()
                for i in range(1, 5):
                    to_sib(i).wait_recv()
                for cp_ in h_copies(1):
                    cp_.start()

        up_phase(3)
        x_copy = pltpu.make_async_copy(x_ref, xo_ref, x_sem)
        x_copy.start()
        out_tail = pltpu.make_async_copy(w_out.at[layer, :, pl.ds(out_full, width - out_full)], wtail, t_sem)
        for j in range(4):
            out_copy(j).start()
        out_tail.start()
        down_phase(3)

        @pl.loop(0, n_out - 4)
        def _(j):
            out_chunk(j, CHUNK)

            @pl.when(j + 4 < n_out - 1)
            def _():
                out_copy(j + 4).start()

            @pl.when(j + 4 == n_out - 1)
            def _():
                out_copy(n_out - 1).start()

        for j in range(n_out - 4, n_out):
            out_chunk(j, min(CHUNK, out_full - j * CHUNK))
        out_tail.wait()
        hb[:rows, out_full:] = jnp.dot(ctx_ref[...], wtail[...], preferred_element_type=F32).astype(BF16)

        for k in (n_dn - 2, n_dn - 1):
            arrive(3, k)
            settle(3, k, (3 * n_dn + k) % 2, False)
            ring_copy(3, k).start()
        x_copy.wait()
        for k in range(n_dn):
            w = CHUNK if k < n_dn - 1 else dn_tail
            cols = slice(k * CHUNK, k * CHUNK + w)
            ring_copy(2, k).wait_recv()
            ring_copy(3, k).wait_recv()
            mlp = sbuf[k, :, :w].astype(F32) + rbuf[1, k, :, :w].astype(F32) + rbuf[2, k, :, :w].astype(F32)
            xo_ref[:, cols] = (xo_ref[:, cols].astype(F32) + hb[:rows, cols].astype(F32) + mlp).astype(BF16)
        for q in range(4):
            k = 4 * n_dn - 4 + q
            sib_copy(k // n_dn, k % n_dn).wait_send()
        for t in (2, 3):
            for k in range(n_dn):
                ring_copy(t, k).wait_send()

    out_full = width // 128 * 128
    n_out = -(-out_full // CHUNK)
    pl.run_scoped(mlp_scope, pltpu.VMEM((ff, width), BF16))
    for i in range(3):
        to_right(i).wait_send()
        to_left(i).wait_send()
    for i in range(5):
        to_sib(i).wait_send()

    if not last:
        @pl.loop(0, rows // 16)
        def _(r):
            band = pl.ds(pl.multiple_of(r * 16, 16), 16)
            values = xo_ref[band, :].astype(F32)
            centered = values - jnp.mean(values, axis=-1, keepdims=True)
            variance = jnp.mean(centered * centered, axis=-1, keepdims=True)
            ho_ref[band, :] = (centered * lax.rsqrt(variance + LN_EPS) * gb_ref[0:1, :] + gb_ref[1:2, :]).astype(BF16)


def pair_stride(width):
    return -(-(-(-width // 128)) // 8) * 8


def layer_block(layer, last, h, positions, cs, x, gb, w_qkv, k_cache, v_cache, w_up, w_down, w_out):
    rows, width = x.shape
    head_dim, seq_len = k_cache.shape[2:]
    ff = w_up.shape[2]
    total = w_qkv.shape[2]
    tail = total - total // CHUNK * CHUNK
    n_up = -(-ff // CHUNK)
    n_dn = -(-width // CHUNK)
    size = lax.axis_size("tp")
    vmem = pl.BlockSpec(memory_space=pltpu.VMEM)
    smem = pl.BlockSpec(memory_space=pltpu.SMEM)
    hbm = pl.BlockSpec(memory_space=pl.ANY)
    row_shape = jax.ShapeDtypeStruct((rows, width), BF16)
    outs = [
        jax.ShapeDtypeStruct((size * rows, width), BF16),
        jax.ShapeDtypeStruct((rows, 2 * head_dim), BF16),
        row_shape,
    ]
    norm_scratch = [pltpu.VMEM((rows, width), BF16)]
    if not last:
        outs.append(row_shape)
        norm_scratch = []
    return pl.pallas_call(
        functools.partial(layer_kernel, layer, last),
        out_shape=outs,
        in_specs=[vmem, smem, vmem, hbm, vmem] + [hbm] * 6,
        out_specs=[hbm] + [vmem] * (len(outs) - 1),
        scratch_shapes=norm_scratch + [
            pltpu.VMEM((width, ff), BF16),
            pltpu.VMEM((width, tail), BF16),
            pltpu.VMEM((rows, 2 * head_dim), F32),
            pltpu.VMEM((2 * rows, width), BF16),
            pltpu.VMEM((2 * rows, ff), BF16),
            pltpu.VMEM((2 * rows, CHUNK), F32),
            pltpu.VMEM((2, rows, CHUNK), F32),
            pltpu.VMEM((4, rows, CHUNK), BF16),
            pltpu.VMEM((2 * n_dn + 1, rows, CHUNK), BF16),
            pltpu.VMEM((3 * n_dn + 1, rows, CHUNK), BF16),
            pltpu.VMEM((3, n_dn, rows, CHUNK), BF16),
            pltpu.SemaphoreType.DMA((QKV_SLOTS,)),
            pltpu.SemaphoreType.DMA,
            pltpu.SemaphoreType.DMA((2, CACHE_SLOTS)),
            pltpu.SemaphoreType.DMA,
            pltpu.SemaphoreType.DMA((2, 3)),
            pltpu.SemaphoreType.DMA((2, 3)),
            pltpu.SemaphoreType.DMA((5,)),
            pltpu.SemaphoreType.DMA((5,)),
            pltpu.SemaphoreType.DMA((n_up,)),
            pltpu.SemaphoreType.DMA((n_dn,)),
            pltpu.SemaphoreType.DMA((2,)),
            pltpu.SemaphoreType.DMA((4,)),
            pltpu.SemaphoreType.DMA,
            pltpu.SemaphoreType.DMA((4,)),
            pltpu.SemaphoreType.DMA((4, n_dn)),
            pltpu.SemaphoreType.DMA((3, n_dn)),
            pltpu.SemaphoreType.DMA((3, n_dn)),
        ],
        compiler_params=pltpu.CompilerParams(
            collective_id=layer, has_side_effects=True, vmem_limit_bytes=67_043_328),
    )(h, positions, cs, x, gb, w_qkv, k_cache, v_cache, w_up, w_down, w_out)


def layer_norm(rows_in, gamma_row, beta_row):
    values = rows_in.astype(F32)
    row_mean = jnp.mean(values, axis=-1, keepdims=True)
    centered = values - row_mean
    variance = jnp.mean(centered * centered, axis=-1, keepdims=True)
    return (centered * lax.rsqrt(variance + LN_EPS) * gamma_row + beta_row).astype(BF16)


def device_layers(hidden, positions, ln_gamma, ln_beta, w_qkv, w_out, w_up, w_down, k_cache, v_cache):
    layers = w_qkv.shape[0]
    seq_len, head_dim = k_cache.shape[2:]
    half_dim = head_dim // 2
    inv_freq = 1.0 / (ROPE_BASE ** (jnp.arange(half_dim, dtype=F32) * (2.0 / head_dim)))
    angles = positions.astype(F32)[:, None] * inv_freq[None, :]
    cos_table = jnp.cos(angles)
    sin_table = jnp.sin(angles)
    cs = jnp.stack([jnp.tile(cos_table, (1, 4)), jnp.tile(jnp.concatenate([-sin_table, sin_table], axis=1), (1, 2))])
    k_turned = jnp.swapaxes(k_cache, 2, 3)
    v_turned = jnp.swapaxes(v_cache, 2, 3)
    x = hidden
    normed = layer_norm(x, ln_gamma[0], ln_beta[0])
    rows_new = []
    for layer in range(layers):
        last = layer == layers - 1
        nxt = layer if last else layer + 1
        gb = jnp.stack([ln_gamma[nxt], ln_beta[nxt]])
        outs = layer_block(layer, last, normed, positions, cs, x, gb, w_qkv, k_turned, v_turned, w_up, w_down, w_out)
        rows_new.append(outs[1])
        x = outs[2]
        if not last:
            normed = outs[3]
    seq_ids = jnp.arange(seq_len, dtype=jnp.int32)
    mask = (seq_ids[None, :] == positions[:, None])[None, :, :, None]
    rows_new = jnp.stack(rows_new)[:, :, None, :]
    k_new = jnp.where(mask, rows_new[..., :head_dim], k_cache)
    v_new = jnp.where(mask, rows_new[..., head_dim:], v_cache)
    return x, k_new, v_new


def solution(mesh):
    row_spec = P(('dp', 'tp'), None)
    cache_spec = P(None, ('dp', 'tp'), None, None)
    in_specs = (row_spec, P(('dp', 'tp')), P(), P(), P(), P(), P(None, None, 'tp'), P(None, 'tp', None), cache_spec, cache_spec)
    return jax.shard_map(device_layers, mesh=mesh, in_specs=in_specs, out_specs=(row_spec, cache_spec, cache_spec), check_vma=False)
```

time: 521 us -> 275 us (0.53)
  matrix products: 275 us -> 0 us
  Pallas kernels: 0 us -> 248 us
  waiting for transfers between devices: 110 us -> 0 us
  local copies, waits for them, and re-layouts: 56.7 us -> 5.49 us
  other arithmetic: 60.8 us -> 20 us
  between operations: 14.4 us -> 0.76 us
    dot_general x12 -> x0, matrix products: 275 us -> none  [the longest x2 110 us: device_layers(): jnp.dot(normed_group, w_up[layer_idx], preferred_element_type=jnp.float32)]
    pallas_call x0 -> x2, Pallas kernels: none -> 248 us  [layer_block(): pl.pallas_call(functools.partial(layer_kernel, layer, last), out_shape=ou...]
    all_gather x2 -> x0, waiting for transfers between devices: 110 us -> none  [device_layers(): normed_group = lax.all_gather(normed, 'tp', axis=0, tiled=True)]
    unnamed x54 -> x10, local copies, waits for them, and re-layouts: 41 us -> 4.23 us
    another operation x4 -> x2, other arithmetic: 21 us -> 1.33 us  [the longest x1 0.67 us: device_layers(): jnp.stack([jnp.tile(cos_table, (1, 4)), jnp.tile(jnp.concatenate([-sin_ta...]
    sub x2 -> x0, other arithmetic: 13.9 us -> none  [local_attention(): probabilities = jax.nn.softmax(scores, axis=-1).astype(jnp.bfloat16)]
    slice x9 -> x1, local copies, waits for them, and re-layouts: 7.96 us -> 0.98 us  [device_layers(): gb = jnp.stack([ln_gamma[nxt], ln_beta[nxt]])]
    convert_element_type x2 -> x0, local copies, waits for them, and re-layouts: 5.95 us -> none  [local_attention(): context.astype(jnp.bfloat16).reshape(rows_n, att_width)]
  transfers between devices with their start and end apart: 4 -> 0, of which waited for: 2 -> 0; matrix products, arithmetic and copies ran while one was open for 28% -> 0% of each run, Pallas kernels for 0% -> 0%
where the time goes in v1:
time: 275 us; the launch traced here: 274 us
  Pallas kernels  248 us (90%)
  other arithmetic  20 us (7%)
  local copies, waits for them, and re-layouts  5.49 us (2%)
    pallas_call x2, Pallas kernels, layer_block(): pl.pallas_call(functools.partial(layer_kernel, layer, last), out_shape=ou...  248 us
    select_n x1, other arithmetic, device_layers(): v_new = jnp.where(mask, rows_new[..., head_dim:], v_cache)  14.3 us

profile of v1, /device:TPU:113, one launch (start us, length us, event | category | flops | bytes accessed | tf_op | source)
XLA Modules:
  0.0 274.3 jit_solution(14656655204954128089)
XLA Ops:
  0.6 0.7 convert_element_type.11
  1.3 1.4 iota_compare_fusion
  2.7 0.1 multiply_cosine_fusion
  2.8 0.1 copy.18
  2.9 0.1 copy.17
  3.0 0.7 pad_maximum_fusion.cs_ref
  3.7 1.0 fusion.7
  4.7 0.7 pad_maximum_fusion.1.gb_ref
  5.3 1.6 copy.16.x_ref
  6.9 0.0 copy-start
  6.9 0.3 convert_reduce_fusion
  7.2 0.5 fusion.2
  7.7 0.3 copy-done
  7.9 1.5 fusion.5.h_ref
  9.5 125.4 %shard_map.121 = (bf16[1024,4544]{1,0:T(8,128)(2,1)}, bf16[128,128]{1,0:T(8,128)(2,1)}, bf16[128,4544]{1,0:T(8,128)(2,1)}, bf16[128,4544]{1,0:T(8,128)(2,1)}) custom-call(bf16[128,4544]{1,0:T(8,128)(2,1)} %fusion.5.h_ref, s32[128]{0:T(128)} %pos_ref.3, f32[2,128,128]{2,1,0:T(8,128)} %pad_maximum_fusion.cs_ref, bf16[128,4544]{1,0:T(8,128)(2,1)} %copy-done, ...), custom_call_target="tpu_custom_call" | custom-call | tf_op jit(solution)/shard_map/pallas_call | solution.py:479
  134.9 122.6 %shard_map.122 = (bf16[1024,4544]{1,0:T(8,128)(2,1)}, bf16[128,128]{1,0:T(8,128)(2,1)}, bf16[128,4544]{1,0:T(8,128)(2,1)}) custom-call(bf16[128,4544]{1,0:T(8,128)(2,1)} %get-tuple-element.8.h_ref, s32[128]{0:T(128)} %pos_ref.3, f32[2,128,128]{2,1,0:T(8,128)} %pad_maximum_fusion.cs_ref, bf16[128,4544]{1,0:T(8,128)(2,1)} %get-tuple-element.9.x_ref, ...), custom_call_target="tpu_custom_call" | custom-call | tf_op jit(solution)/shard_map/pallas_call | solution.py:479
  257.5 0.0 copy-start.2
  257.5 0.0 copy-start.3
  257.5 0.0 copy-start.1
  257.5 2.4 copy.20
  259.9 0.0 copy-done.2
  259.9 0.0 copy-done.3
  259.9 0.1 slice_bitcast_fusion
  260.0 0.0 copy-done.1
  260.0 14.3 %broadcast_select_fusion = (bf16[2,128,256,64]{2,3,1,0:T(8,128)(2,1)}, bf16[2,128,256,64]{2,3,1,0:T(8,128)(2,1)}) fusion(bf16[2,128,256,64]{2,3,1,0:T(8,128)(2,1)} %param.19, pred[128,256]{1,0:T(8,128)(4,1)S(1)} %copy-done.1, bf16[2,128,64]{2,1,0:T(8,128)(2,1)S(1)} %get-tuple-element.19, bf16[2,128,256,64]{2,3,1,0:T(8,128)(2,1)} %param.18, ...), kind=kLoop, calls=%fused_computation | loop fusion | flops 8388608 | bytes 33652736 | tf_op jit(solution)/shard_map/jit(_where)/select_n | solution.py:554
  (7 shorter events, 0.0 us)
Async XLA Ops:
  6.9 1.0 copy-start
  257.5 2.4 copy-start.2
  257.5 2.4 copy-start.3
  257.5 2.5 copy-start.1

commit v2 on v1

--- a/solution.py
+++ b/solution.py
@@ -149,8 +149,6 @@
         for i in range(CACHE_SLOTS):
             for cp_ in cache_copies(i):
                 cp_.start()
-        for j in range(n_up):
-            up_copy(j, CHUNK if j < n_up - 1 else up_tail).start()
         out = qkv_chunk(n_chunks - 1)
         turned = None
         for i in range(pairs):
@@ -199,6 +197,23 @@
                     cp_.start()
 
 
+        def out_copy(j):
+            slot = j % QKV_SLOTS if isinstance(j, int) else lax.rem(j, QKV_SLOTS)
+            w = min(CHUNK, out_full - j * CHUNK) if isinstance(j, int) else CHUNK
+            return pltpu.make_async_copy(
+                w_out.at[layer, :, span(j, CHUNK, w)], wbuf.at[slot, :, pl.ds(0, w)], o_sem.at[slot])
+
+        def out_chunk(j, w):
+            slot = j % QKV_SLOTS if isinstance(j, int) else lax.rem(j, QKV_SLOTS)
+            out_copy(j).wait()
+            attn = jnp.dot(ctx_ref[...], wbuf[slot, :, :w], preferred_element_type=F32)
+            xo_ref[:, span(j, CHUNK, w)] = attn.astype(BF16)
+
+        out_tail = pltpu.make_async_copy(w_out.at[layer, :, pl.ds(out_full, width - out_full)], wtail, t_sem)
+        for j in range(QKV_SLOTS):
+            out_copy(j).start()
+        out_tail.start()
+
         @pl.loop(0, n_blocks)
         def _(i):
             @pl.when(i == 1)
@@ -208,12 +223,40 @@
                 to_left(0).wait_recv()
                 to_left(2).start()
 
+            @pl.when(i == n_blocks // 2)
+            def _():
+                for j in range(n_up):
+                    up_copy(j, CHUNK if j < n_up - 1 else up_tail).start()
+
             attend(i)
 
         for m in range(-(-width // 128)):
             w = min(128, width - 128 * m)
             ctx_ref[:, 128 * m:128 * m + w] = qp[pl.ds(m, rows, stride), :][:, :w].astype(BF16)
 
+        to_right(1).wait_recv()
+        to_sib(1).start()
+        to_left(1).wait_recv()
+        to_sib(2).start()
+
+        @pl.loop(0, n_out - 1)
+        def _(j):
+            out_chunk(j, CHUNK)
+
+            @pl.when(j + QKV_SLOTS < n_out - 1)
+            def _():
+                out_copy(j + QKV_SLOTS).start()
+
+            @pl.when(j + QKV_SLOTS == n_out - 1)
+            def _():
+                out_copy(n_out - 1).start()
+
+        out_chunk(n_out - 1, out_full - (n_out - 1) * CHUNK)
+        out_tail.wait()
+        xo_ref[:, out_full:] = jnp.dot(ctx_ref[...], wtail[...], preferred_element_type=F32).astype(BF16)
+
+    out_full = width // 128 * 128
+    n_out = -(-out_full // CHUNK)
     pl.run_scoped(
         attention_scope,
         pltpu.VMEM((QKV_SLOTS, width, CHUNK), BF16),
@@ -222,10 +265,6 @@
         pltpu.VMEM((CACHE_SLOTS, ROW_BLOCK, head_dim, seq_len), BF16),
     )
 
-    to_right(1).wait_recv()
-    to_sib(1).start()
-    to_left(1).wait_recv()
-    to_sib(2).start()
     own_copy.wait()
     to_sib(0).wait_recv()
 
@@ -235,14 +274,15 @@
             return pltpu.make_async_copy(w_down.at[layer, :, cols], wdn.at[:, cols], d_sem.at[k])
 
         def h_copies(t):
-            off = jnp.where(t == 0, 0, jnp.where(t == 1, 2, jnp.where(t == 2, 1, chips - 1)))
-            dest = lax.rem(chip + off, chips)
-            first = pl.multiple_of((2 * dest + core) * rows, rows)
-            second = pl.multiple_of((2 * dest + 1 - core) * rows, rows)
-            return (
-                pltpu.make_async_copy(hg.at[pl.ds(first, rows)], hb.at[pl.ds(0, rows)], h_sem.at[0]),
-                pltpu.make_async_copy(hg.at[pl.ds(second, rows)], hb.at[pl.ds(rows, rows)], h_sem.at[1]),
-            )
+            copies = []
+            for i in range(4):
+                own = core if i < 2 else 1 - core
+                side = jnp.where(t == 0, 0, jnp.where(t == 1, 2, 1 if i % 2 == 0 else chips - 1))
+                which = jnp.where(t < 2, i % 2, t - 2)
+                start = (2 * lax.rem(chip + side, chips) + own) * rows + which * half
+                copies.append(pltpu.make_async_copy(
+                    hg.at[pl.ds(pl.multiple_of(start, half), half)], hb.at[pl.ds(i * half, half)], h_sem.at[i]))
+            return copies
 
         def sib_copy(t, k):
             slot = lax.rem(t * n_dn + k, 4)
@@ -254,12 +294,18 @@
         def sums(t):
             return jnp.where(t == 3, 1, t)
 
-        def ring_copy(t, k):
-            goes_right = jnp.logical_or(t == 2, jnp.logical_and(t == 1, k >= n_left))
-            return pltpu.make_async_remote_copy(
-                src_ref=sbuf.at[sums(t) * n_dn + k], dst_ref=rbuf.at[t - 1, k],
-                send_sem=is_sem.at[t - 1, k], recv_sem=ir_sem.at[t - 1, k],
-                device_id={"tp": jnp.where(goes_right, right, left)}, device_id_type=pl.DeviceIdType.MESH)
+        def far_copy(k):
+            return remote(sbuf.at[n_dn + k], rbuf.at[0, k], is_sem.at[0, k], ir_sem.at[0, k],
+                          jnp.where(k >= n_left, right, left))
+
+        def near_copies(t, k):
+            which = t - 2
+            rows_to = pl.ds(pl.multiple_of(which * half, half), half)
+            return [
+                remote(sbuf.at[sums(t) * n_dn + k, pl.ds(i * half, half)], rbuf.at[1 + i, k, rows_to],
+                       is_sem.at[1 + 2 * i + which, k], ir_sem.at[1 + 2 * i + which, k], to)
+                for i, to in enumerate((right, left))
+            ]
 
         def up_phase(t):
             for cp in h_copies(t):
@@ -293,16 +339,19 @@
 
         def arrive(t, k):
             sib_copy(t, k).wait_recv()
-            relay = jnp.logical_or(jnp.logical_and(t == 2, k >= n_left), jnp.logical_and(t == 3, k < n_left))
-
-            @pl.when(relay)
-            def _():
-                ring_copy(1, k).wait_recv()
-                mine[lax.rem(t * n_dn + k, 2)] += rbuf[0, k].astype(F32)
+            @pl.when(t == 2)
+            def _():
+                far_copy(k).wait_recv()
+
+            @pl.when(t >= 2)
+            def _():
+                on = pl.ds(pl.multiple_of(jnp.where(k >= n_left, 0, half), half), half)
+                of = pl.ds(pl.multiple_of((t - 2) * half, half), half)
+                mine[lax.rem(t * n_dn + k, 2), on] += rbuf[0, k, of].astype(F32)
 
             @pl.when(t == 3)
             def _():
-                ring_copy(1, k).wait_send()
+                far_copy(k).wait_send()
 
         def settle(t, k, slot, spare):
             to = jnp.where(spare, 3 * n_dn, sums(t) * n_dn + k)
@@ -337,9 +386,14 @@
                 sib_send[lax.rem(q, 4), :, :w] = out[rows:].astype(BF16)
                 sib_copy(t, k).start()
 
-                @pl.when(jnp.logical_and(q >= 2, pt > 0))
+                @pl.when(jnp.logical_and(q >= 2, pt == 1))
                 def _():
-                    ring_copy(pt, pk).start()
+                    far_copy(pk).start()
+
+                @pl.when(pt >= 2)
+                def _():
+                    for cp_ in near_copies(pt, pk):
+                        cp_.start()
 
             @pl.loop(0, n_dn - 1)
             def _(k):
@@ -347,18 +401,6 @@
 
             step(n_dn - 1, dn_tail)
 
-
-        def out_copy(j):
-            slot = j % 4 if isinstance(j, int) else lax.rem(j, 4)
-            w = min(CHUNK, out_full - j * CHUNK) if isinstance(j, int) else CHUNK
-            return pltpu.make_async_copy(
-                w_out.at[layer, :, span(j, CHUNK, w)], wup.at[:, span(slot, CHUNK, w)], o_sem.at[slot])
-
-        def out_chunk(j, w):
-            slot = j % 4 if isinstance(j, int) else lax.rem(j, 4)
-            out_copy(j).wait()
-            attn = jnp.dot(ctx_ref[...], wup[:, span(slot, CHUNK, w)], preferred_element_type=F32)
-            hb[:rows, span(j, CHUNK, w)] = attn.astype(BF16)
 
         for cp_ in h_copies(0):
             cp_.start()
@@ -387,52 +429,31 @@
                     cp_.start()
 
         up_phase(3)
-        x_copy = pltpu.make_async_copy(x_ref, xo_ref, x_sem)
+        x_copy = pltpu.make_async_copy(x_ref, ctx_ref, x_sem)
         x_copy.start()
-        out_tail = pltpu.make_async_copy(w_out.at[layer, :, pl.ds(out_full, width - out_full)], wtail, t_sem)
-        for j in range(4):
-            out_copy(j).start()
-        out_tail.start()
         down_phase(3)
-
-        @pl.loop(0, n_out - 4)
-        def _(j):
-            out_chunk(j, CHUNK)
-
-            @pl.when(j + 4 < n_out - 1)
-            def _():
-                out_copy(j + 4).start()
-
-            @pl.when(j + 4 == n_out - 1)
-            def _():
-                out_copy(n_out - 1).start()
-
-        for j in range(n_out - 4, n_out):
-            out_chunk(j, min(CHUNK, out_full - j * CHUNK))
-        out_tail.wait()
-        hb[:rows, out_full:] = jnp.dot(ctx_ref[...], wtail[...], preferred_element_type=F32).astype(BF16)
 
         for k in (n_dn - 2, n_dn - 1):
             arrive(3, k)
             settle(3, k, (3 * n_dn + k) % 2, False)
-            ring_copy(3, k).start()
+            for cp_ in near_copies(3, k):
+                cp_.start()
         x_copy.wait()
         for k in range(n_dn):
             w = CHUNK if k < n_dn - 1 else dn_tail
             cols = slice(k * CHUNK, k * CHUNK + w)
-            ring_copy(2, k).wait_recv()
-            ring_copy(3, k).wait_recv()
+            for cp_ in near_copies(2, k) + near_copies(3, k):
+                cp_.wait_recv()
             mlp = sbuf[k, :, :w].astype(F32) + rbuf[1, k, :, :w].astype(F32) + rbuf[2, k, :, :w].astype(F32)
-            xo_ref[:, cols] = (xo_ref[:, cols].astype(F32) + hb[:rows, cols].astype(F32) + mlp).astype(BF16)
+            xo_ref[:, cols] = (ctx_ref[:, cols].astype(F32) + xo_ref[:, cols].astype(F32) + mlp).astype(BF16)
         for q in range(4):
             k = 4 * n_dn - 4 + q
             sib_copy(k // n_dn, k % n_dn).wait_send()
         for t in (2, 3):
             for k in range(n_dn):
-                ring_copy(t, k).wait_send()
-
-    out_full = width // 128 * 128
-    n_out = -(-out_full // CHUNK)
+                for cp_ in near_copies(t, k):
+                    cp_.wait_send()
+
     pl.run_scoped(mlp_scope, pltpu.VMEM((ff, width), BF16))
     for i in range(3):
         to_right(i).wait_send()
@@ -503,13 +524,13 @@
             pltpu.SemaphoreType.DMA((5,)),
             pltpu.SemaphoreType.DMA((n_up,)),
             pltpu.SemaphoreType.DMA((n_dn,)),
-            pltpu.SemaphoreType.DMA((2,)),
             pltpu.SemaphoreType.DMA((4,)),
+            pltpu.SemaphoreType.DMA((QKV_SLOTS,)),
             pltpu.SemaphoreType.DMA,
             pltpu.SemaphoreType.DMA((4,)),
             pltpu.SemaphoreType.DMA((4, n_dn)),
-            pltpu.SemaphoreType.DMA((3, n_dn)),
-            pltpu.SemaphoreType.DMA((3, n_dn)),
+            pltpu.SemaphoreType.DMA((5, n_dn)),
+            pltpu.SemaphoreType.DMA((5, n_dn)),
         ],
         compiler_params=pltpu.CompilerParams(
             collective_id=layer, has_side_effects=True, vmem_limit_bytes=67_043_328),

time: 275 us -> 285 us (1.036)
  Pallas kernels: 248 us -> 258 us
    pallas_call x2, Pallas kernels: 248 us -> 258 us  [layer_block(): pl.pallas_call(functools.partial(layer_kernel, layer, last), out_shape=ou...]
where the time goes in v2:
time: 285 us; the launch traced here: 284 us
  Pallas kernels  258 us (91%)
  other arithmetic  20 us (7%)
  local copies, waits for them, and re-layouts  5.49 us (2%)
    pallas_call x2, Pallas kernels, layer_block(): pl.pallas_call(functools.partial(layer_kernel, layer, last), out_shape=ou...  258 us
    select_n x1, other arithmetic, device_layers(): v_new = jnp.where(mask, rows_new[..., head_dim:], v_cache)  14.3 us

profile of v2, /device:TPU:113, one launch (start us, length us, event | category | flops | bytes accessed | tf_op | source)
XLA Modules:
  0.0 284.1 jit_solution(4927952372596390531)
XLA Ops:
  0.6 0.7 convert_element_type.11
  1.3 1.4 iota_compare_fusion
  2.7 0.1 multiply_cosine_fusion
  2.8 0.1 copy.18
  2.9 0.1 copy.17
  3.0 0.7 pad_maximum_fusion.cs_ref
  3.7 1.0 fusion.7
  4.7 0.7 pad_maximum_fusion.1.gb_ref
  5.3 1.6 copy.16.x_ref
  6.9 0.0 copy-start
  6.9 0.3 convert_reduce_fusion
  7.2 0.5 fusion.2
  7.7 0.3 copy-done
  7.9 1.5 fusion.5.h_ref
  9.5 131.8 %shard_map.121 = (bf16[1024,4544]{1,0:T(8,128)(2,1)}, bf16[128,128]{1,0:T(8,128)(2,1)}, bf16[128,4544]{1,0:T(8,128)(2,1)}, bf16[128,4544]{1,0:T(8,128)(2,1)}) custom-call(bf16[128,4544]{1,0:T(8,128)(2,1)} %fusion.5.h_ref, s32[128]{0:T(128)} %pos_ref.3, f32[2,128,128]{2,1,0:T(8,128)} %pad_maximum_fusion.cs_ref, bf16[128,4544]{1,0:T(8,128)(2,1)} %copy-done, ...), custom_call_target="tpu_custom_call" | custom-call | tf_op jit(solution)/shard_map/pallas_call | solution.py:500
  141.2 126.1 %shard_map.122 = (bf16[1024,4544]{1,0:T(8,128)(2,1)}, bf16[128,128]{1,0:T(8,128)(2,1)}, bf16[128,4544]{1,0:T(8,128)(2,1)}) custom-call(bf16[128,4544]{1,0:T(8,128)(2,1)} %get-tuple-element.8.h_ref, s32[128]{0:T(128)} %pos_ref.3, f32[2,128,128]{2,1,0:T(8,128)} %pad_maximum_fusion.cs_ref, bf16[128,4544]{1,0:T(8,128)(2,1)} %get-tuple-element.9.x_ref, ...), custom_call_target="tpu_custom_call" | custom-call | tf_op jit(solution)/shard_map/pallas_call | solution.py:500
  267.3 0.0 copy-start.2
  267.3 0.0 copy-start.3
  267.4 0.0 copy-start.1
  267.4 2.4 copy.20
  269.7 0.0 copy-done.2
  269.7 0.0 copy-done.3
  269.8 0.1 slice_bitcast_fusion
  269.9 0.0 copy-done.1
  269.9 14.3 %broadcast_select_fusion = (bf16[2,128,256,64]{2,3,1,0:T(8,128)(2,1)}, bf16[2,128,256,64]{2,3,1,0:T(8,128)(2,1)}) fusion(bf16[2,128,256,64]{2,3,1,0:T(8,128)(2,1)} %param.19, pred[128,256]{1,0:T(8,128)(4,1)S(1)} %copy-done.1, bf16[2,128,64]{2,1,0:T(8,128)(2,1)S(1)} %get-tuple-element.19, bf16[2,128,256,64]{2,3,1,0:T(8,128)(2,1)} %param.18, ...), kind=kLoop, calls=%fused_computation | loop fusion | flops 8388608 | bytes 33652736 | tf_op jit(solution)/shard_map/jit(_where)/select_n | solution.py:575
  (7 shorter events, 0.0 us)
Async XLA Ops:
  6.9 1.0 copy-start
  267.3 2.4 copy-start.2
  267.3 2.4 copy-start.3
  267.4 2.5 copy-start.1

commit v3 on v1

--- a/solution.py
+++ b/solution.py
@@ -235,14 +235,15 @@
             return pltpu.make_async_copy(w_down.at[layer, :, cols], wdn.at[:, cols], d_sem.at[k])
 
         def h_copies(t):
-            off = jnp.where(t == 0, 0, jnp.where(t == 1, 2, jnp.where(t == 2, 1, chips - 1)))
-            dest = lax.rem(chip + off, chips)
-            first = pl.multiple_of((2 * dest + core) * rows, rows)
-            second = pl.multiple_of((2 * dest + 1 - core) * rows, rows)
-            return (
-                pltpu.make_async_copy(hg.at[pl.ds(first, rows)], hb.at[pl.ds(0, rows)], h_sem.at[0]),
-                pltpu.make_async_copy(hg.at[pl.ds(second, rows)], hb.at[pl.ds(rows, rows)], h_sem.at[1]),
-            )
+            copies = []
+            for i in range(4):
+                own = core if i < 2 else 1 - core
+                side = jnp.where(t == 0, 0, jnp.where(t == 1, 2, 1 if i % 2 == 0 else chips - 1))
+                which = jnp.where(t < 2, i % 2, t - 2)
+                start = (2 * lax.rem(chip + side, chips) + own) * rows + which * half
+                copies.append(pltpu.make_async_copy(
+                    hg.at[pl.ds(pl.multiple_of(start, half), half)], hb.at[pl.ds(i * half, half)], h_sem.at[i]))
+            return copies
 
         def sib_copy(t, k):
             slot = lax.rem(t * n_dn + k, 4)
@@ -254,12 +255,18 @@
         def sums(t):
             return jnp.where(t == 3, 1, t)
 
-        def ring_copy(t, k):
-            goes_right = jnp.logical_or(t == 2, jnp.logical_and(t == 1, k >= n_left))
-            return pltpu.make_async_remote_copy(
-                src_ref=sbuf.at[sums(t) * n_dn + k], dst_ref=rbuf.at[t - 1, k],
-                send_sem=is_sem.at[t - 1, k], recv_sem=ir_sem.at[t - 1, k],
-                device_id={"tp": jnp.where(goes_right, right, left)}, device_id_type=pl.DeviceIdType.MESH)
+        def far_copy(k):
+            return remote(sbuf.at[n_dn + k], rbuf.at[0, k], is_sem.at[0, k], ir_sem.at[0, k],
+                          jnp.where(k >= n_left, right, left))
+
+        def near_copies(t, k):
+            which = t - 2
+            rows_to = pl.ds(pl.multiple_of(which * half, half), half)
+            return [
+                remote(sbuf.at[sums(t) * n_dn + k, pl.ds(i * half, half)], rbuf.at[1 + i, k, rows_to],
+                       is_sem.at[1 + 2 * i + which, k], ir_sem.at[1 + 2 * i + which, k], to)
+                for i, to in enumerate((right, left))
+            ]
 
         def up_phase(t):
             for cp in h_copies(t):
@@ -293,16 +300,19 @@
 
         def arrive(t, k):
             sib_copy(t, k).wait_recv()
-            relay = jnp.logical_or(jnp.logical_and(t == 2, k >= n_left), jnp.logical_and(t == 3, k < n_left))
-
-            @pl.when(relay)
-            def _():
-                ring_copy(1, k).wait_recv()
-                mine[lax.rem(t * n_dn + k, 2)] += rbuf[0, k].astype(F32)
+            @pl.when(t == 2)
+            def _():
+                far_copy(k).wait_recv()
+
+            @pl.when(t >= 2)
+            def _():
+                on = pl.ds(pl.multiple_of(jnp.where(k >= n_left, 0, half), half), half)
+                of = pl.ds(pl.multiple_of((t - 2) * half, half), half)
+                mine[lax.rem(t * n_dn + k, 2), on] += rbuf[0, k, of].astype(F32)
 
             @pl.when(t == 3)
             def _():
-                ring_copy(1, k).wait_send()
+                far_copy(k).wait_send()
 
         def settle(t, k, slot, spare):
             to = jnp.where(spare, 3 * n_dn, sums(t) * n_dn + k)
@@ -337,9 +347,14 @@
                 sib_send[lax.rem(q, 4), :, :w] = out[rows:].astype(BF16)
                 sib_copy(t, k).start()
 
-                @pl.when(jnp.logical_and(q >= 2, pt > 0))
+                @pl.when(jnp.logical_and(q >= 2, pt == 1))
                 def _():
-                    ring_copy(pt, pk).start()
+                    far_copy(pk).start()
+
+                @pl.when(pt >= 2)
+                def _():
+                    for cp_ in near_copies(pt, pk):
+                        cp_.start()
 
             @pl.loop(0, n_dn - 1)
             def _(k):
@@ -415,13 +430,14 @@
         for k in (n_dn - 2, n_dn - 1):
             arrive(3, k)
             settle(3, k, (3 * n_dn + k) % 2, False)
-            ring_copy(3, k).start()
+            for cp_ in near_copies(3, k):
+                cp_.start()
         x_copy.wait()
         for k in range(n_dn):
             w = CHUNK if k < n_dn - 1 else dn_tail
             cols = slice(k * CHUNK, k * CHUNK + w)
-            ring_copy(2, k).wait_recv()
-            ring_copy(3, k).wait_recv()
+            for cp_ in near_copies(2, k) + near_copies(3, k):
+                cp_.wait_recv()
             mlp = sbuf[k, :, :w].astype(F32) + rbuf[1, k, :, :w].astype(F32) + rbuf[2, k, :, :w].astype(F32)
             xo_ref[:, cols] = (xo_ref[:, cols].astype(F32) + hb[:rows, cols].astype(F32) + mlp).astype(BF16)
         for q in range(4):
@@ -429,7 +445,8 @@
             sib_copy(k // n_dn, k % n_dn).wait_send()
         for t in (2, 3):
             for k in range(n_dn):
-                ring_copy(t, k).wait_send()
+                for cp_ in near_copies(t, k):
+                    cp_.wait_send()
 
     out_full = width // 128 * 128
     n_out = -(-out_full // CHUNK)
@@ -503,13 +520,13 @@
             pltpu.SemaphoreType.DMA((5,)),
             pltpu.SemaphoreType.DMA((n_up,)),
             pltpu.SemaphoreType.DMA((n_dn,)),
-            pltpu.SemaphoreType.DMA((2,)),
+            pltpu.SemaphoreType.DMA((4,)),
             pltpu.SemaphoreType.DMA((4,)),
             pltpu.SemaphoreType.DMA,
             pltpu.SemaphoreType.DMA((4,)),
             pltpu.SemaphoreType.DMA((4, n_dn)),
-            pltpu.SemaphoreType.DMA((3, n_dn)),
-            pltpu.SemaphoreType.DMA((3, n_dn)),
+            pltpu.SemaphoreType.DMA((5, n_dn)),
+            pltpu.SemaphoreType.DMA((5, n_dn)),
         ],
         compiler_params=pltpu.CompilerParams(
             collective_id=layer, has_side_effects=True, vmem_limit_bytes=67_043_328),

time: 275 us -> 262 us (0.953)
  Pallas kernels: 248 us -> 236 us
    pallas_call x2, Pallas kernels: 248 us -> 236 us  [layer_block(): pl.pallas_call(functools.partial(layer_kernel, layer, last), out_shape=ou...]
where the time goes in v3:
time: 262 us
  Pallas kernels  236 us (90%)
  other arithmetic  20 us (8%)
  local copies, waits for them, and re-layouts  5.49 us (2%)
    pallas_call x2, Pallas kernels, layer_block(): pl.pallas_call(functools.partial(layer_kernel, layer, last), out_shape=ou...  236 us
    select_n x1, other arithmetic, device_layers(): v_new = jnp.where(mask, rows_new[..., head_dim:], v_cache)  14.3 us

profile of v3, /device:TPU:113, one launch (start us, length us, event | category | flops | bytes accessed | tf_op | source)
XLA Modules:
  0.0 262.0 jit_solution(4034128488820070334)
XLA Ops:
  0.6 0.7 convert_element_type.11
  1.3 1.4 iota_compare_fusion
  2.7 0.1 multiply_cosine_fusion
  2.8 0.1 copy.18
  2.9 0.1 copy.17
  3.0 0.7 pad_maximum_fusion.cs_ref
  3.7 1.0 fusion.7
  4.7 0.7 pad_maximum_fusion.1.gb_ref
  5.3 1.6 copy.16.x_ref
  6.9 0.0 copy-start
  6.9 0.3 convert_reduce_fusion
  7.2 0.5 fusion.2
  7.7 0.3 copy-done
  7.9 1.5 fusion.5.h_ref
  9.5 120.7 %shard_map.121 = (bf16[1024,4544]{1,0:T(8,128)(2,1)}, bf16[128,128]{1,0:T(8,128)(2,1)}, bf16[128,4544]{1,0:T(8,128)(2,1)}, bf16[128,4544]{1,0:T(8,128)(2,1)}) custom-call(bf16[128,4544]{1,0:T(8,128)(2,1)} %fusion.5.h_ref, s32[128]{0:T(128)} %pos_ref.3, f32[2,128,128]{2,1,0:T(8,128)} %pad_maximum_fusion.cs_ref, bf16[128,4544]{1,0:T(8,128)(2,1)} %copy-done, ...), custom_call_target="tpu_custom_call" | custom-call | tf_op jit(solution)/shard_map/pallas_call | solution.py:496
  130.2 114.9 %shard_map.122 = (bf16[1024,4544]{1,0:T(8,128)(2,1)}, bf16[128,128]{1,0:T(8,128)(2,1)}, bf16[128,4544]{1,0:T(8,128)(2,1)}) custom-call(bf16[128,4544]{1,0:T(8,128)(2,1)} %get-tuple-element.8.h_ref, s32[128]{0:T(128)} %pos_ref.3, f32[2,128,128]{2,1,0:T(8,128)} %pad_maximum_fusion.cs_ref, bf16[128,4544]{1,0:T(8,128)(2,1)} %get-tuple-element.9.x_ref, ...), custom_call_target="tpu_custom_call" | custom-call | tf_op jit(solution)/shard_map/pallas_call | solution.py:496
  245.2 0.0 copy-start.2
  245.2 0.0 copy-start.3
  245.2 0.0 copy-start.1
  245.2 2.4 copy.20
  247.6 0.0 copy-done.2
  247.6 0.0 copy-done.3
  247.6 0.1 slice_bitcast_fusion
  247.7 0.0 copy-done.1
  247.7 14.3 %broadcast_select_fusion = (bf16[2,128,256,64]{2,3,1,0:T(8,128)(2,1)}, bf16[2,128,256,64]{2,3,1,0:T(8,128)(2,1)}) fusion(bf16[2,128,256,64]{2,3,1,0:T(8,128)(2,1)} %param.19, pred[128,256]{1,0:T(8,128)(4,1)S(1)} %copy-done.1, bf16[2,128,64]{2,1,0:T(8,128)(2,1)S(1)} %get-tuple-element.19, bf16[2,128,256,64]{2,3,1,0:T(8,128)(2,1)} %param.18, ...), kind=kLoop, calls=%fused_computation | loop fusion | flops 8388608 | bytes 33652736 | tf_op jit(solution)/shard_map/jit(_where)/select_n | solution.py:571
  (7 shorter events, 0.0 us)
Async XLA Ops:
  6.9 1.0 copy-start
  245.2 2.4 copy-start.2
  245.2 2.4 copy-start.3
  245.2 2.5 copy-start.1
